TPU v7x, 128 devices: a whole 4x4x4 slice. The times are simulated.
128 devices in a mesh: keys: 32 (over x, z, core), heads: 4 (over y).
Axes of the slice: x: 4, y: 4, z: 4, core: 2. Of those that a mesh axis runs over, the one named last changes fastest.
Arguments:
- queries: bfloat16 [64, 64, 128], P(None, 'heads'), may hold values from -128 to 128
- keys: bfloat16 [524288, 8, 128], P('keys', 'heads'), may hold values from -4 to 4
- values: bfloat16 [524288, 8, 128], P('keys', 'heads'), may hold values from -6 to 6
- out_weight: bfloat16 [8192, 8192], P('heads', 'keys'), may hold values from -0.0625 to 0.0625
- probe: bfloat16 [8192], P('keys'), may hold values from -6 to 6
- knocked: int32 [64, 16], replicated, may hold values from 0 to 127
Outputs:
- readout: float32 [64, 128], P(None, 'keys')
- picked: float32 [64, 16], replicated
All inputs are finite; a program needn't handle non-finite values.
Results may differ from a plain program's by a relative error of at most 0.0003.
Values sent between devices are 32-bit elements; how exact they have to be, the bound alone decides.
No kernel may reach another device: no remote copies, remote signals or barrier semaphores. Data moves between devices by JAX's collectives and lax.ppermute only.
A program may use at most 128 MiB of HBM per device.

v0:
```python
import jax
import jax.numpy as jnp
from jax import lax
from jax.sharding import PartitionSpec as P

BLOCK = 4096


NEG = -1e30


def total_of_pieces(x, axis):
    blocks = lax.all_gather(x, axis)
    return blocks.sum(axis=0)


def sent_together(arrays, axis, dim, along):
    widths = [a.shape[along] for a in arrays]
    both = jnp.concatenate(arrays, axis=along)
    out = lax.all_gather(both, axis, axis=dim, tiled=True)
    return tuple(jnp.split(out, [sum(widths[:k]) for k in range(1, len(widths))], axis=along))


def copy_for_each(x, axis):
    size = lax.axis_size(axis)
    return lax.all_to_all(jnp.broadcast_to(x[None], (size, *x.shape)), axis, 0, 0, tiled=True)


def of_everyone(x, axis):
    everything = copy_for_each(x, axis)
    return jnp.sum(everything, axis=0)


def combine(first, second):
    m1, s1, o1 = first
    m2, s2, o2 = second
    top = jnp.maximum(m1, m2)
    a = jnp.exp(m1 - top)
    b = jnp.exp(m2 - top)
    return (top, s1 * a + s2 * b, o1 * a + o2 * b)


def masked_total(stacked, chosen):
    peaks, totals, summed = stacked
    flags = chosen.reshape((-1,) + (1,) * (peaks.ndim - 1))
    top = jnp.max(jnp.where(flags, peaks, NEG), axis=0)
    factor = jnp.where(flags, jnp.exp(peaks - top[None]), 0.0)
    return (top, jnp.sum(factor * totals, axis=0), jnp.sum(factor * summed, axis=0))


def body(queries, keys, values, out_weight, probe, knocked):
    nq, hq, hd = queries.shape
    kvh = keys.shape[1]
    group = hq // kvh
    nblk = keys.shape[0] // BLOCK
    lanes = lax.axis_size("keys")
    device = lax.axis_index("keys")
    context = keys.shape[0] * lanes
    direction = total_of_pieces(
        jnp.dot(out_weight, probe, preferred_element_type=jnp.float32), "keys"
    )
    direction = direction.reshape(kvh, group, hd)
    grouped = queries.reshape(nq, kvh, group, hd)
    key_blocks = keys.reshape(nblk, BLOCK, kvh, hd)
    value_blocks = values.reshape(nblk, BLOCK, kvh, hd)
    query_pos = context - nq + jnp.arange(nq, dtype=jnp.int32)

    def block_state(inputs):
        kblk, vblk, local = inputs
        scores = jnp.einsum(
            "qgrd,kgd->qgrk", grouped, kblk, preferred_element_type=jnp.float32
        ) * hd ** (-0.5)
        key_pos = (device * nblk + local) * BLOCK + jnp.arange(BLOCK, dtype=jnp.int32)
        allowed = key_pos[None, :] <= query_pos[:, None]
        scores = jnp.where(allowed[:, None, None, :], scores, NEG)
        top = jnp.max(scores, axis=-1)
        weights = jnp.exp(scores - top[..., None])
        total = jnp.sum(weights, axis=-1)
        summed = jnp.einsum(
            "qgrk,kgd->qgrd", weights.astype(jnp.bfloat16), vblk, preferred_element_type=jnp.float32
        )
        summed = jnp.sum(summed * direction, axis=-1)
        return (top, total, summed)

    states = lax.map(block_state, (key_blocks, value_blocks, jnp.arange(nblk, dtype=jnp.int32)))
    empty = (
        jnp.full(states[0].shape[1:], NEG, jnp.float32),
        jnp.zeros(states[1].shape[1:], jnp.float32),
        jnp.zeros(states[2].shape[1:], jnp.float32),
    )

    def member(index):
        return (states[0][index], states[1][index], states[2][index])

    inner_before = [empty]
    for index in range(nblk - 1):
        inner_before.append(combine(inner_before[-1], member(index)))
    inner_after = [empty]
    for index in range(nblk - 1, 0, -1):
        inner_after.insert(0, combine(member(index), inner_after[0]))
    device_total = combine(inner_before[-1], member(nblk - 1))
    stacked = sent_together(
        (device_total[0][None], device_total[1][None], device_total[2][None]), "keys", 0, 1
    )
    order = jnp.arange(lanes, dtype=jnp.int32)
    before = masked_total(stacked, order < device)
    after = masked_total(stacked, order > device)
    columns = []
    for index in range(nblk):
        state = combine(combine(before, inner_before[index]), combine(inner_after[index], after))
        top, total, summed = state
        columns.append(jnp.sum(summed / total, axis=(1, 2)))
    partial_read = jnp.stack(columns, axis=1)
    readout = of_everyone(partial_read, "heads")
    global_ids = device * nblk + jnp.arange(nblk, dtype=jnp.int32)
    matches = knocked[:, :, None] == global_ids[None, None, :]
    local_pick = jnp.sum(jnp.where(matches, readout[:, None, :], 0.0), axis=-1)
    picked = of_everyone(local_pick, "keys")
    return (readout, picked)


def solution(mesh):
    in_specs = (
        P(None, "heads", None),
        P("keys", "heads", None),
        P("keys", "heads", None),
        P("heads", "keys"),
        P("keys"),
        P(),
    )
    out_specs = (P(None, "keys"), P())
    return jax.shard_map(body, mesh=mesh, in_specs=in_specs, out_specs=out_specs, check_vma=False)
```

profile of v0, /device:TPU:1, one launch (start us, length us, event | category | flops | bytes accessed | tf_op | source)
XLA Modules:
  0.0 207.5 jit_solution(2528802314306885912)
XLA Ops:
  0.6 0.0 copy-start
  0.7 1.1 copy.28
  1.8 0.7 reshape.69
  2.5 0.0 copy-done
  2.5 0.4 fusion.104
  2.8 27.5 %all-gather = f32[65536]{0:T(1024)S(1)} all-gather(f32[2048]{0:T(1024)S(1)} %bitcast.407), channel_id=2, replica_groups=mesh['keys'=32,'heads'=4] {'keys'}, dimensions={0}, use_global_device_ids=true | all-gather | bytes 270336 | tf_op jit(solution)/shard_map/all_gather | solution.py:13
  30.5 0.0 copy-start.2
  30.5 126.5 %while.17 = (s32[]{:T(128)}, f32[4,64,2,8]{1,3,2,0:T(8,128)S(1)}, f32[4,64,2,8]{1,3,2,0:T(8,128)S(1)}, f32[4,64,2,8]{1,3,2,0:T(8,128)S(1)}, s32[4]{0:T(128)S(1)}...) while((s32[]{:T(128)}, f32[4,64,2,8]{1,3,2,0:T(8,128)S(1)}, ...), condition=%wide.region_5.6_spmd.clone, body=%wide.region_1.5_spmd.clone.sunk | while | flops 2194146304 | bytes 64336564 | solution.py:85
  30.5 0.6 dynamic_slice.27
  31.7 0.2 broadcast_compare_fusion.2
  32.0 3.3 %constant_dynamic-slice_fusion.4 = bf16[1,4096,2,128]{3,2,1,0:T(2,128)(2,1)S(1)} fusion(bf16[4,4096,2,128]{3,2,1,0:T(2,128)(2,1)} %get-tuple-element.318, s32[]{:T(128)S(6)} %copy.63), kind=kLoop, calls=%fused_computation.20.clone.1 | loop fusion | bytes 4194308 | tf_op jit(solution)/shard_map/while/body/jit(dynamic_index_in_dim)/dynamic_slice | solution.py:85
  35.2 7.6 %fusion.115 = (f32[64,2,8]{0,2,1:T(8,128)S(1)}, f32[2,4096,64,8]{1,2,3,0:T(8,128)}) fusion(pred[64,4096]{1,0:T(8,128)(4,1)S(1)} %broadcast_compare_fusion.2, bf16[64,2,8,128]{3,0,2,1:T(8,128)(2,1)S(1)} %get-tuple-element.319, bf16[1,4096,2,128]{3,2,1,0:T(2,128)(2,1)S(1)} %constant_dynamic-slice_fusion.4), kind=kOutput, calls=%fused_computation.5.clone.1 | convolution fusion | flops 1086323712 | bytes 19402752 | tf_op jit(solution)/shard_map/while/body/eval_jaxpr/qgrd,kgd->qgrk/dot_general | solution.py:70
  42.8 3.2 %constant_dynamic-slice_fusion.5 = bf16[1,4096,2,128]{3,2,1,0:T(2,128)(2,1)S(1)} fusion(bf16[4,4096,2,128]{3,2,1,0:T(2,128)(2,1)} %get-tuple-element.320, s32[]{:T(128)S(6)} %copy.63), kind=kLoop, calls=%fused_computation.19.clone.1 | loop fusion | bytes 4194308 | tf_op jit(solution)/shard_map/while/body/jit(dynamic_index_in_dim)/dynamic_slice | solution.py:85
  46.0 7.8 %fusion.116 = f32[64,2,8]{0,2,1:T(8,128)S(1)} fusion(f32[2,4096,64,8]{1,2,3,0:T(8,128)} %get-tuple-element.285, f32[64,2,8]{0,2,1:T(8,128)S(1)} %get-tuple-element.284, pred[64,4096]{1,0:T(8,128)(4,1)S(1)} %broadcast_compare_fusion.2, bf16[1,4096,2,128]{3,2,1,0:T(2,128)(2,1)S(1)} %constant_dynamic-slice_fusion.5, f32[2,8,128]{2,1,0:T(8,128)S(1)} %bitcast.408), kind=kOutput, calls=%fused_computation.13.clone.1 | convolution fusion | flops 1090780160 | bytes 19152896 | tf_op jit(solution)/shard_map/while/body/eval_jaxpr/qgrk,kgd->qgrd/dot_general | solution.py:79
  53.8 8.2 %fusion.117 = f32[64,2,8]{0,2,1:T(8,128)S(1)} fusion(f32[2,4096,64,8]{1,2,3,0:T(8,128)} %get-tuple-element.285, f32[64,2,8]{0,2,1:T(8,128)S(1)} %get-tuple-element.284, pred[64,4096]{1,0:T(8,128)(4,1)S(1)} %broadcast_compare_fusion.2), kind=kLoop, calls=%fused_computation.4.clone.1 | loop fusion | flops 16776192 | bytes 17047552 | tf_op jit(solution)/shard_map/while/body/eval_jaxpr/reduce_sum | solution.py:78
  62.1 0.6 dynamic_slice.27
  63.3 0.2 broadcast_compare_fusion.2
  63.6 3.3 %constant_dynamic-slice_fusion.4 = bf16[1,4096,2,128]{3,2,1,0:T(2,128)(2,1)S(1)} fusion(bf16[4,4096,2,128]{3,2,1,0:T(2,128)(2,1)} %get-tuple-element.318, s32[]{:T(128)S(6)} %copy.63), kind=kLoop, calls=%fused_computation.20.clone.1 | loop fusion | bytes 4194308 | tf_op jit(solution)/shard_map/while/body/jit(dynamic_index_in_dim)/dynamic_slice | solution.py:85
  66.8 7.6 %fusion.115 = (f32[64,2,8]{0,2,1:T(8,128)S(1)}, f32[2,4096,64,8]{1,2,3,0:T(8,128)}) fusion(pred[64,4096]{1,0:T(8,128)(4,1)S(1)} %broadcast_compare_fusion.2, bf16[64,2,8,128]{3,0,2,1:T(8,128)(2,1)S(1)} %get-tuple-element.319, bf16[1,4096,2,128]{3,2,1,0:T(2,128)(2,1)S(1)} %constant_dynamic-slice_fusion.4), kind=kOutput, calls=%fused_computation.5.clone.1 | convolution fusion | flops 1086323712 | bytes 19402752 | tf_op jit(solution)/shard_map/while/body/eval_jaxpr/qgrd,kgd->qgrk/dot_general | solution.py:70
  74.4 3.2 %constant_dynamic-slice_fusion.5 = bf16[1,4096,2,128]{3,2,1,0:T(2,128)(2,1)S(1)} fusion(bf16[4,4096,2,128]{3,2,1,0:T(2,128)(2,1)} %get-tuple-element.320, s32[]{:T(128)S(6)} %copy.63), kind=kLoop, calls=%fused_computation.19.clone.1 | loop fusion | bytes 4194308 | tf_op jit(solution)/shard_map/while/body/jit(dynamic_index_in_dim)/dynamic_slice | solution.py:85
  77.7 7.8 %fusion.116 = f32[64,2,8]{0,2,1:T(8,128)S(1)} fusion(f32[2,4096,64,8]{1,2,3,0:T(8,128)} %get-tuple-element.285, f32[64,2,8]{0,2,1:T(8,128)S(1)} %get-tuple-element.284, pred[64,4096]{1,0:T(8,128)(4,1)S(1)} %broadcast_compare_fusion.2, bf16[1,4096,2,128]{3,2,1,0:T(2,128)(2,1)S(1)} %constant_dynamic-slice_fusion.5, f32[2,8,128]{2,1,0:T(8,128)S(1)} %bitcast.408), kind=kOutput, calls=%fused_computation.13.clone.1 | convolution fusion | flops 1090780160 | bytes 19152896 | tf_op jit(solution)/shard_map/while/body/eval_jaxpr/qgrk,kgd->qgrd/dot_general | solution.py:79
  85.4 8.2 %fusion.117 = f32[64,2,8]{0,2,1:T(8,128)S(1)} fusion(f32[2,4096,64,8]{1,2,3,0:T(8,128)} %get-tuple-element.285, f32[64,2,8]{0,2,1:T(8,128)S(1)} %get-tuple-element.284, pred[64,4096]{1,0:T(8,128)(4,1)S(1)} %broadcast_compare_fusion.2), kind=kLoop, calls=%fused_computation.4.clone.1 | loop fusion | flops 16776192 | bytes 17047552 | tf_op jit(solution)/shard_map/while/body/eval_jaxpr/reduce_sum | solution.py:78
  93.7 0.6 dynamic_slice.27
  95.0 0.2 broadcast_compare_fusion.2
  95.2 3.3 %constant_dynamic-slice_fusion.4 = bf16[1,4096,2,128]{3,2,1,0:T(2,128)(2,1)S(1)} fusion(bf16[4,4096,2,128]{3,2,1,0:T(2,128)(2,1)} %get-tuple-element.318, s32[]{:T(128)S(6)} %copy.63), kind=kLoop, calls=%fused_computation.20.clone.1 | loop fusion | bytes 4194308 | tf_op jit(solution)/shard_map/while/body/jit(dynamic_index_in_dim)/dynamic_slice | solution.py:85
  98.4 7.6 %fusion.115 = (f32[64,2,8]{0,2,1:T(8,128)S(1)}, f32[2,4096,64,8]{1,2,3,0:T(8,128)}) fusion(pred[64,4096]{1,0:T(8,128)(4,1)S(1)} %broadcast_compare_fusion.2, bf16[64,2,8,128]{3,0,2,1:T(8,128)(2,1)S(1)} %get-tuple-element.319, bf16[1,4096,2,128]{3,2,1,0:T(2,128)(2,1)S(1)} %constant_dynamic-slice_fusion.4), kind=kOutput, calls=%fused_computation.5.clone.1 | convolution fusion | flops 1086323712 | bytes 19402752 | tf_op jit(solution)/shard_map/while/body/eval_jaxpr/qgrd,kgd->qgrk/dot_general | solution.py:70
  106.0 3.2 %constant_dynamic-slice_fusion.5 = bf16[1,4096,2,128]{3,2,1,0:T(2,128)(2,1)S(1)} fusion(bf16[4,4096,2,128]{3,2,1,0:T(2,128)(2,1)} %get-tuple-element.320, s32[]{:T(128)S(6)} %copy.63), kind=kLoop, calls=%fused_computation.19.clone.1 | loop fusion | bytes 4194308 | tf_op jit(solution)/shard_map/while/body/jit(dynamic_index_in_dim)/dynamic_slice | solution.py:85
  109.3 7.8 %fusion.116 = f32[64,2,8]{0,2,1:T(8,128)S(1)} fusion(f32[2,4096,64,8]{1,2,3,0:T(8,128)} %get-tuple-element.285, f32[64,2,8]{0,2,1:T(8,128)S(1)} %get-tuple-element.284, pred[64,4096]{1,0:T(8,128)(4,1)S(1)} %broadcast_compare_fusion.2, bf16[1,4096,2,128]{3,2,1,0:T(2,128)(2,1)S(1)} %constant_dynamic-slice_fusion.5, f32[2,8,128]{2,1,0:T(8,128)S(1)} %bitcast.408), kind=kOutput, calls=%fused_computation.13.clone.1 | convolution fusion | flops 1090780160 | bytes 19152896 | tf_op jit(solution)/shard_map/while/body/eval_jaxpr/qgrk,kgd->qgrd/dot_general | solution.py:79
  117.1 8.2 %fusion.117 = f32[64,2,8]{0,2,1:T(8,128)S(1)} fusion(f32[2,4096,64,8]{1,2,3,0:T(8,128)} %get-tuple-element.285, f32[64,2,8]{0,2,1:T(8,128)S(1)} %get-tuple-element.284, pred[64,4096]{1,0:T(8,128)(4,1)S(1)} %broadcast_compare_fusion.2), kind=kLoop, calls=%fused_computation.4.clone.1 | loop fusion | flops 16776192 | bytes 17047552 | tf_op jit(solution)/shard_map/while/body/eval_jaxpr/reduce_sum | solution.py:78
  125.3 0.6 dynamic_slice.27
  126.6 0.2 broadcast_compare_fusion.2
  126.8 3.3 %constant_dynamic-slice_fusion.4 = bf16[1,4096,2,128]{3,2,1,0:T(2,128)(2,1)S(1)} fusion(bf16[4,4096,2,128]{3,2,1,0:T(2,128)(2,1)} %get-tuple-element.318, s32[]{:T(128)S(6)} %copy.63), kind=kLoop, calls=%fused_computation.20.clone.1 | loop fusion | bytes 4194308 | tf_op jit(solution)/shard_map/while/body/jit(dynamic_index_in_dim)/dynamic_slice | solution.py:85
  130.0 7.6 %fusion.115 = (f32[64,2,8]{0,2,1:T(8,128)S(1)}, f32[2,4096,64,8]{1,2,3,0:T(8,128)}) fusion(pred[64,4096]{1,0:T(8,128)(4,1)S(1)} %broadcast_compare_fusion.2, bf16[64,2,8,128]{3,0,2,1:T(8,128)(2,1)S(1)} %get-tuple-element.319, bf16[1,4096,2,128]{3,2,1,0:T(2,128)(2,1)S(1)} %constant_dynamic-slice_fusion.4), kind=kOutput, calls=%fused_computation.5.clone.1 | convolution fusion | flops 1086323712 | bytes 19402752 | tf_op jit(solution)/shard_map/while/body/eval_jaxpr/qgrd,kgd->qgrk/dot_general | solution.py:70
  137.6 3.2 %constant_dynamic-slice_fusion.5 = bf16[1,4096,2,128]{3,2,1,0:T(2,128)(2,1)S(1)} fusion(bf16[4,4096,2,128]{3,2,1,0:T(2,128)(2,1)} %get-tuple-element.320, s32[]{:T(128)S(6)} %copy.63), kind=kLoop, calls=%fused_computation.19.clone.1 | loop fusion | bytes 4194308 | tf_op jit(solution)/shard_map/while/body/jit(dynamic_index_in_dim)/dynamic_slice | solution.py:85
  140.9 7.8 %fusion.116 = f32[64,2,8]{0,2,1:T(8,128)S(1)} fusion(f32[2,4096,64,8]{1,2,3,0:T(8,128)} %get-tuple-element.285, f32[64,2,8]{0,2,1:T(8,128)S(1)} %get-tuple-element.284, pred[64,4096]{1,0:T(8,128)(4,1)S(1)} %broadcast_compare_fusion.2, bf16[1,4096,2,128]{3,2,1,0:T(2,128)(2,1)S(1)} %constant_dynamic-slice_fusion.5, f32[2,8,128]{2,1,0:T(8,128)S(1)} %bitcast.408), kind=kOutput, calls=%fused_computation.13.clone.1 | convolution fusion | flops 1090780160 | bytes 19152896 | tf_op jit(solution)/shard_map/while/body/eval_jaxpr/qgrk,kgd->qgrd/dot_general | solution.py:79
  148.7 8.2 %fusion.117 = f32[64,2,8]{0,2,1:T(8,128)S(1)} fusion(f32[2,4096,64,8]{1,2,3,0:T(8,128)} %get-tuple-element.285, f32[64,2,8]{0,2,1:T(8,128)S(1)} %get-tuple-element.284, pred[64,4096]{1,0:T(8,128)(4,1)S(1)} %broadcast_compare_fusion.2), kind=kLoop, calls=%fused_computation.4.clone.1 | loop fusion | flops 16776192 | bytes 17047552 | tf_op jit(solution)/shard_map/while/body/eval_jaxpr/reduce_sum | solution.py:78
  157.0 0.1 pad_maximum_fusion
  157.1 24.2 %all_gather.11 = f32[32,192,2,8]{1,3,2,0:T(8,128)S(1)} all-gather(f32[1,192,2,8]{1,3,2,0:T(8,128)S(1)} %pad_maximum_fusion), channel_id=1, replica_groups=mesh['keys'=32,'heads'=4] {'keys'}, dimensions={0}, use_global_device_ids=true | all-gather | bytes 405504 | tf_op jit(solution)/shard_map/all_gather | solution.py:20
  181.2 0.1 select_reduce_fusion.1
  181.3 0.2 multiply_reduce_fusion.3
  181.5 0.2 multiply_reduce_fusion.2
  181.8 0.1 fusion.100
  181.9 0.1 fusion.103
  181.9 0.7 reshape.71
  182.6 4.2 %all-to-all-start = ((f32[4,1,256]{2,1,0:T(1,128)}), f32[4,1,256]{2,1,0:T(1,128)S(1)}, u32[]{:S(2)}, u32[]{:S(2)}) async-start(f32[4,1,256]{2,1,0:T(1,128)} %reshape.71), calls=%async_computation | async-start | bytes 8192 | tf_op jit(solution)/shard_map/all_to_all | solution.py:26
  186.8 4.1 %all-to-all-done = f32[4,1,256]{2,1,0:T(1,128)S(1)} async-done(((f32[4,1,256]{2,1,0:T(1,128)}), f32[4,1,256]{2,1,0:T(1,128)S(1)}, u32[]{:S(2)}, u32[]{:S(2)}) %all-to-all-start) | async-done | bytes 4128 | tf_op jit(solution)/shard_map/all_to_all | solution.py:26
  191.0 0.5 broadcast.100
  191.5 0.7 reduce
  192.1 0.1 reshape.72
  192.2 0.0 copy-done.2
  192.2 0.0 copy-start.1
  192.3 0.1 select_reduce_fusion.2
  192.4 0.2 reshape.73
  192.5 13.2 %all_to_all.10 = f32[32,1,1024]{2,1,0:T(1,128)S(1)} all-to-all(f32[32,1,1024]{2,1,0:T(1,128)S(1)} %reshape.73), channel_id=1, replica_groups=mesh['keys'=32,'heads'=4] {'keys'}, dimensions={0} | all-to-all | bytes 262144 | tf_op jit(solution)/shard_map/all_to_all | solution.py:26
  205.8 1.0 reduce.1
  206.7 0.1 reshape.74
  206.8 0.6 bitcast_reduce_fusion
  207.5 0.0 copy-done.1
  (32 shorter events, 0.4 us)
Async XLA Ops:
  0.6 1.8 copy-start
  30.5 161.8 %copy-start.2 = (s32[64,16]{0,1:T(8,128)S(1)}, s32[64,16]{0,1:T(8,128)}, u32[]{:S(2)}) copy-start(s32[64,16]{0,1:T(8,128)} %param.13) | copy-start | bytes 12292
  182.6 8.3 %all-to-all-start = ((f32[4,1,256]{2,1,0:T(1,128)}), f32[4,1,256]{2,1,0:T(1,128)S(1)}, u32[]{:S(2)}, u32[]{:S(2)}) async-start(f32[4,1,256]{2,1,0:T(1,128)} %reshape.71), calls=%async_computation | async-start | bytes 8192 | tf_op jit(solution)/shard_map/all_to_all | solution.py:26
  192.2 15.2 %copy-start.1 = (f32[64,4]{0,1:T(4,128)}, f32[64,4]{0,1:T(4,128)S(1)}, u32[]{:S(2)}) copy-start(f32[64,4]{0,1:T(4,128)S(1)} %bitcast_reduce_fusion.1) | copy-start | bytes 3076
where the time goes:
time: 208 us; the launch traced here: 207 us
  blocking collectives  64.9 us (31%)
  matrix products  61.8 us (30%)
  other arithmetic  37.1 us (18%)
  local copies, waits for them, and re-layouts  31.7 us (15%)
  starting transfers between devices  4.19 us (2%)
  waiting for transfers between devices  4.14 us (2%)
  loops' own time  2.81 us (1%)
    reduce_sum x4, other arithmetic, block_state(): total = jnp.sum(weights, axis=-1)  33 us
    dot_general x4, matrix products, block_state(): jnp.einsum('qgrk,kgd->qgrd', weights.astype(jnp.bfloat16), vblk, preferre...  31.1 us
    dot_general x4, matrix products, block_state(): jnp.einsum('qgrd,kgd->qgrk', grouped, kblk, preferred_element_type=jnp.fl...  30.3 us
    dynamic_slice x12, local copies, waits for them, and re-layouts, body(): lax.map(block_state, (key_blocks, value_blocks, jnp.arange(nblk, dtype=jn...  28.3 us
    all_gather x1, blocking collectives, total_of_pieces(): blocks = lax.all_gather(x, axis)  27.5 us
    all_gather x1, blocking collectives, sent_together(): out = lax.all_gather(both, axis, axis=dim, tiled=True)  24.2 us
    all_to_all x1, blocking collectives, copy_for_each(): lax.all_to_all(jnp.broadcast_to(x[None], (size, *x.shape)), axis, 0, 0, t...  13.2 us
    all_to_all x1, starting transfers between devices, copy_for_each(): lax.all_to_all(jnp.broadcast_to(x[None], (size, *x.shape)), axis, 0, 0, t...  4.19 us
  transfers between devices with their start and end apart: 1, of which 1 were waited for; matrix products, arithmetic and copies ran while one was open for 0% of the time, Pallas kernels for 0%

commit v1 on v0

v1 whole, which is shorter than its diff:
```python
import functools

import jax
import jax.numpy as jnp
from jax import lax
from jax.experimental import pallas as pl
from jax.experimental.pallas import tpu as pltpu
from jax.sharding import Mesh, PartitionSpec as P

BLOCK = 4096
KEY_AXES = (4, 4, 2)
NEG = -1e30
SCALE2 = 128 ** -0.5 * 1.4426950408889634
HIGH = lax.Precision.HIGHEST
F32 = jnp.float32


def attn_kernel(base_ref, q_ref, k_ref, v_ref, ms_ref, o_ref, qt, sc, *, T1, T2, nblk, context, nq):
    b = pl.program_id(0)
    rows = k_ref.shape[0]
    R = qt.shape[1]
    hd = k_ref.shape[1]
    @pl.when(b == 0)
    def _():
        q = q_ref[...].astype(jnp.float32)
        g = q.shape[1] // 2
        both = jnp.concatenate([q[:, :g].reshape(R, hd), q[:, g:].reshape(R, hd)], axis=1)
        qt[...] = both.T.astype(jnp.bfloat16)

    def masked(x):
        par = lax.broadcasted_iota(jnp.int32, x.shape, 0) & 1
        even = (par == 0).astype(x.dtype)
        return jnp.concatenate([x * even, x * (1 - even)], axis=1)

    def first(i, mx):
        at = pl.ds(pl.multiple_of(i * T1, T1), T1)
        s = jnp.dot(masked(k_ref[at, :]), qt[...], preferred_element_type=jnp.float32)
        sc[at, :] = s
        return jnp.maximum(mx, jnp.max(s.reshape(T1 // 8, 8, R), axis=0))

    mx = lax.fori_loop(0, rows // T1, first, jnp.full((8, R), NEG, jnp.float32))
    tail = pl.ds(rows - 2 * nq, 2 * nq)

    @pl.when(base_ref[0] + (b + 1) * (rows // 2) == context)
    def _():
        s = sc[tail, :]
        key = lax.shift_right_logical(lax.broadcasted_iota(jnp.int32, s.shape, 0), 1)
        query = lax.div(lax.broadcasted_iota(jnp.int32, s.shape, 1), jnp.int32(R // nq))
        sc[tail, :] = jnp.where(key <= query, s, NEG)
    last = base_ref[0] + (b + 1) * (rows // 2) == context
    def fix(_):
        def again(i, mx):
            at = pl.ds(pl.multiple_of(i * 128, 128), 128)
            return jnp.maximum(mx, jnp.max(sc[at, :].reshape(16, 8, R), axis=0))
        return lax.fori_loop(0, rows // 128, again, jnp.full((8, R), NEG, jnp.float32))
    mx = lax.cond(last, fix, lambda _: mx, 0)
    mx = jnp.maximum(mx, pltpu.roll(mx, 2, 0))
    mx = jnp.maximum(mx, pltpu.roll(mx, 4, 0))

    o_ref[...] = jnp.zeros_like(o_ref)
    def second(i, tot):
        at = pl.ds(pl.multiple_of(i * T2, T2), T2)
        s = sc[at, :].reshape(T2 // 8, 8, R)
        p = jnp.exp2((s - mx[None]) * SCALE2)
        tot = tot + jnp.sum(p, axis=0)
        pb = p.reshape(T2, R).astype(jnp.bfloat16)
        o_ref[...] += lax.dot_general(masked(v_ref[at, :]), pb, (((0,), (0,)), ((), ())), preferred_element_type=jnp.float32)
        return tot
    tot = lax.fori_loop(0, rows // T2, second, jnp.zeros((8, R), jnp.float32))
    tot = tot + pltpu.roll(tot, 2, 0)
    tot = tot + pltpu.roll(tot, 4, 0)
    ms_ref[0:2, :] = mx[0:2] * SCALE2
    ms_ref[2:4, :] = tot[0:2]

def attention(base, queries, keys, values, block, context, T1=512, T2=512, interpret=False):
    nq, hq, hd = queries.shape
    n, kvh, _ = keys.shape
    R = nq * hq // kvh
    nblk = n // block
    rows = kvh * block
    k2 = keys.reshape(n * kvh, hd)
    v2 = values.reshape(n * kvh, hd)
    return pl.pallas_call(
        functools.partial(attn_kernel, T1=T1, T2=T2, nblk=nblk, context=context, nq=nq),
        grid=(nblk,),
        in_specs=[
            pl.BlockSpec(memory_space=pltpu.SMEM),
            pl.BlockSpec((nq, hq, hd), lambda b: (0, 0, 0)),
            pl.BlockSpec((rows, hd), lambda b: (b, 0)),
            pl.BlockSpec((rows, hd), lambda b: (b, 0)),
        ],
        out_specs=[
            pl.BlockSpec((None, 4, R), lambda b: (b, 0, 0)),
            pl.BlockSpec((None, kvh * hd, R), lambda b: (b, 0, 0)),
        ],
        out_shape=[
            jax.ShapeDtypeStruct((nblk, 4, R), jnp.float32),
            jax.ShapeDtypeStruct((nblk, kvh * hd, R), jnp.float32),
        ],
        scratch_shapes=[
            pltpu.VMEM((kvh * hd, R), jnp.bfloat16),
            pltpu.VMEM((rows, R), jnp.float32),
        ],
        compiler_params=pltpu.CompilerParams(vmem_limit_bytes=60 * 2**20),
        cost_estimate=pl.CostEstimate(flops=4 * R * n * kvh * hd * 2, bytes_accessed=2 * n * kvh * hd * 2, transcendentals=R * n * kvh),
        name="attention",
    )(base, queries, k2, v2)


def iota(shape, dim):
    return lax.broadcasted_iota(jnp.int32, shape, dim)


def direction_kernel(w_ref, p_ref, out_ref):
    part = lax.dot_general(p_ref[...], w_ref[...], (((1,), (1,)), ((), ())), preferred_element_type=F32)
    heads, hd = out_ref.shape[1:]
    rows = [part[0:1, h * hd:(h + 1) * hd] for h in range(heads)]
    full = jnp.concatenate(rows, axis=0)
    for dest in range(out_ref.shape[0]):
        out_ref[dest] = full


def direction_parts(out_weight, probe, hd, dests):
    rows, cols = out_weight.shape
    probe8 = jnp.broadcast_to(probe[None], (8, cols))
    return pl.pallas_call(
        direction_kernel,
        out_shape=jax.ShapeDtypeStruct((dests, rows // hd, hd), F32),
        cost_estimate=pl.CostEstimate(flops=2 * rows * cols, bytes_accessed=rows * cols * 2, transcendentals=0),
        name="direction",
    )(out_weight, probe8)


def pack_kernel(dir_ref, ms_ref, o_ref, out_ref, x):
    nblk, rows, R = o_ref.shape
    heads, hd = dir_ref.shape[1:]
    group = heads // 2
    direction = jnp.sum(dir_ref[...], axis=0)
    spread = (iota((group, 128), 1) & (group - 1)) == iota((group, 128), 0)
    spread = spread.astype(F32)
    for g in range(2):
        wide = lax.dot_general(direction[g * group:(g + 1) * group], spread, (((0,), (0,)), ((), ())),
                               preferred_element_type=F32, precision=HIGH)
        for b in range(nblk):
            at = g * nblk + b
            x[at:at + 1, :] = ms_ref[b, g:g + 1, :]
            x[8 + at:9 + at, :] = ms_ref[b, 2 + g:3 + g, :]
            for c in range(0, R, 128):
                part = o_ref[b, g * hd:(g + 1) * hd, c:c + 128] * wide
                x[16 + at:17 + at, c:c + 128] = jnp.sum(part, axis=0, keepdims=True)
    dests = out_ref.shape[0]
    share = R // 128
    for dest in range(dests):
        c = dest // (dests // share) * 128
        out_ref[dest] = x[:, c:c + 128]


def pack(gathered, ms, o):
    dests = gathered.shape[0]
    return pl.pallas_call(
        pack_kernel,
        out_shape=jax.ShapeDtypeStruct((dests, 24, 128), F32),
        scratch_shapes=[pltpu.VMEM((24, ms.shape[2]), F32)],
        cost_estimate=pl.CostEstimate(flops=2 * o.size, bytes_accessed=o.size * 4, transcendentals=0),
        name="pack",
    )(gathered, ms, o)


def turned(x, k):
    row = iota(x.shape, x.ndim - 2) & 3
    return jnp.where(row >= k, pltpu.roll(x, k, x.ndim - 2), pltpu.roll(x, k + 4, x.ndim - 2))


def around(x, op):
    x = op(x, turned(x, 1))
    return op(x, turned(x, 2))


def out_of_sources(x):
    n = x.shape[0]
    before = [jnp.zeros_like(x[0])]
    after = [jnp.zeros_like(x[0])]
    for k in range(n - 1):
        before.append(before[-1] + x[k])
        after.insert(0, after[0] + x[n - 1 - k])
    return jnp.stack([p + q for p, q in zip(before, after)], axis=0)


def leave_kernel(got_ref, out_ref):
    m = got_ref[:, 0:8, :]
    s = got_ref[:, 8:16, :]
    o = got_ref[:, 16:24, :]
    n = m.shape[0]
    top = around(jnp.max(m, axis=0), jnp.maximum)
    is_top = m == top[None]
    count = around(jnp.sum(is_top.astype(F32), axis=0), jnp.add)
    second = around(jnp.max(jnp.where(is_top, NEG, m), axis=0), jnp.maximum)
    factor = jnp.exp2(m - top[None])
    low = jnp.where(is_top, 0.0, jnp.exp2(jnp.minimum(m - second[None], 0.0)))
    alone = is_top & (count == 1.0)[None]

    def left_out(x):
        a = x * factor
        inner = turned(a, 1) + turned(a, 2) + turned(a, 3)
        shared = inner + out_of_sources(a + inner)
        rest = around(jnp.sum(x * low, axis=0), jnp.add)
        return jnp.where(alone, rest[None], shared)

    ratio = left_out(o) / left_out(s)
    both = ratio + pltpu.roll(ratio, 4, 1)
    pairs = both.reshape(n // 2, 2, 8, 128)
    dense = jnp.where(iota((n // 2, 8, 128), 1) < 4, pairs[:, 0], pairs[:, 1]).reshape(n * 4, 128)
    queries = out_ref.shape[1]
    per = 128 // queries
    pick = lax.div(iota((queries, 128), 1), jnp.int32(per)) == iota((queries, 128), 0)
    part = lax.dot_general(pick.astype(F32), dense, (((1,), (1,)), ((), ())), preferred_element_type=F32, precision=HIGH)
    for dest in range(out_ref.shape[0]):
        out_ref[dest] = part


def leave(got, queries, dests):
    return pl.pallas_call(
        leave_kernel,
        out_shape=jax.ShapeDtypeStruct((dests, queries, got.shape[0] * 4), F32),
        cost_estimate=pl.CostEstimate(flops=8 * got.size, bytes_accessed=got.size * 4, transcendentals=got.size),
        name="leave",
    )(got)


def finish_kernel(device_ref, got_ref, knocked_ref, read_ref, pick_ref, table):
    nx, ny, q, nb = got_ref.shape
    for i in range(nx):
        total = got_ref[i, 0]
        for j in range(1, ny):
            total = total + got_ref[i, j]
        table[i * q:(i + 1) * q, :] = total
    full = table[...].T
    block = iota(full.shape, 0)
    for k in range(pick_ref.shape[0]):
        here = jnp.where(block == knocked_ref[k:k + 1, :], full, 0.0)
        pick_ref[k:k + 1, :] = jnp.sum(here, axis=0, keepdims=True)
    nblk = read_ref.shape[0]
    for t in range(nblk):
        here = jnp.where(block == device_ref[0] * nblk + t, full, 0.0)
        read_ref[t:t + 1, :] = jnp.sum(here, axis=0, keepdims=True)


def finish(device, got, knocked_t, nblk):
    nx, ny, q, nb = got.shape
    vmem = pl.BlockSpec(memory_space=pltpu.VMEM)
    return pl.pallas_call(
        finish_kernel,
        in_specs=[pl.BlockSpec(memory_space=pltpu.SMEM), vmem, vmem],
        out_specs=[vmem, vmem],
        out_shape=[jax.ShapeDtypeStruct((nblk, nx * q), F32), jax.ShapeDtypeStruct(knocked_t.shape, F32)],
        scratch_shapes=[pltpu.VMEM((nx * q, nb), F32)],
        name="finish",
    )(device, got, knocked_t)


def body(queries, keys, values, out_weight, probe, knocked):
    nq, hq, hd = queries.shape
    nblk = keys.shape[0] // BLOCK
    axes = ("x", "z", "core")
    lanes = lax.axis_size(axes)
    device = lax.axis_index(axes).reshape(1)
    context = keys.shape[0] * lanes
    parts = direction_parts(out_weight, probe, hd, lanes)
    gathered = lax.all_to_all(parts, axes, 0, 0, tiled=True)
    ms, o = attention(device * keys.shape[0], queries, keys, values, BLOCK, context, 4096, 4096)
    got = lax.all_to_all(pack(gathered, ms, o), axes, 0, 0, tiled=True)
    nx, ny = lax.axis_size("x"), lax.axis_size("heads")
    sent = leave(got, nq // nx, nx * ny)
    back = lax.all_to_all(sent, ("x", "heads"), 0, 0, tiled=True)
    read, picked = finish(device, back.reshape(nx, ny, *back.shape[1:]), knocked.T, nblk)
    return read.T, picked.T


def solution(mesh):
    inner = Mesh(mesh.devices.reshape(*KEY_AXES, mesh.devices.shape[1]), ("x", "z", "core", "heads"))
    keys = ("x", "z", "core")
    in_specs = (
        P(None, "heads", None),
        P(keys, "heads", None),
        P(keys, "heads", None),
        P("heads", keys),
        P(keys),
        P(),
    )
    out_specs = (P(None, keys), P())
    return jax.shard_map(body, mesh=inner, in_specs=in_specs, out_specs=out_specs, check_vma=False)
```

time: 208 us -> 82 us (0.39)
  matrix products: 61.8 us -> 0 us
  Pallas kernels: 0 us -> 39.2 us
  other arithmetic: 37.1 us -> 0 us
  blocking collectives: 64.9 us -> 30.1 us
  local copies, waits for them, and re-layouts: 31.7 us -> 1.94 us
  starting transfers between devices: 4.19 us -> 9.42 us
  waiting for transfers between devices: 4.14 us -> 0.01 us
  loops' own time: 2.81 us -> 0 us
    dot_general x9 -> x0, matrix products: 61.8 us -> none  [the longest x4 31.1 us: block_state(): jnp.einsum('qgrk,kgd->qgrd', weights.astype(jnp.bfloat16), vblk, preferre...]
    all_gather x2 -> x0, blocking collectives: 51.7 us -> none  [the longest x1 27.5 us: total_of_pieces(): blocks = lax.all_gather(x, axis)]
    pallas_call x0 -> x5, Pallas kernels: none -> 39.2 us  [the longest x1 29.9 us: attention(): pl.pallas_call(functools.partial(attn_kernel, T1=T1, T2=T2, nblk=nblk, co...]
    reduce_sum x14 -> x0, other arithmetic: 34.3 us -> none  [the longest x4 33 us: block_state(): total = jnp.sum(weights, axis=-1)]
    dynamic_slice x12 -> x0, local copies, waits for them, and re-layouts: 28.3 us -> none  [body(): lax.map(block_state, (key_blocks, value_blocks, jnp.arange(nblk, dtype=jn...]
    all_to_all x1 -> x2, blocking collectives: 13.2 us -> 30.1 us  [the longest x1 18.2 us: body(): got = lax.all_to_all(pack(gathered, ms, o), axes, 0, 0, tiled=True)]
    all_to_all x1, starting transfers between devices: 4.19 us -> 9.42 us  [body(): gathered = lax.all_to_all(parts, axes, 0, 0, tiled=True)]
    all_to_all x1, waiting for transfers between devices: 4.14 us -> 0.01 us  [body(): gathered = lax.all_to_all(parts, axes, 0, 0, tiled=True)]
  transfers between devices with their start and end apart: 1 -> 1, of which waited for: 1 -> 0; matrix products, arithmetic and copies ran while one was open for 0% -> 0% of each run, Pallas kernels for 0% -> 37%
where the time goes in v1:
time: 82 us; the launch traced here: 81.4 us
  Pallas kernels  39.2 us (48%)
  blocking collectives  30.1 us (37%)
  starting transfers between devices  9.42 us (11%)
  local copies, waits for them, and re-layouts  1.94 us (2%)
    pallas_call x1, Pallas kernels, attention(): pl.pallas_call(functools.partial(attn_kernel, T1=T1, T2=T2, nblk=nblk, co...  29.9 us
    all_to_all x1, blocking collectives, body(): got = lax.all_to_all(pack(gathered, ms, o), axes, 0, 0, tiled=True)  18.2 us
    all_to_all x1, blocking collectives, body(): back = lax.all_to_all(sent, ('x', 'heads'), 0, 0, tiled=True)  11.9 us
    all_to_all x1, starting transfers between devices, body(): gathered = lax.all_to_all(parts, axes, 0, 0, tiled=True)  9.42 us
    pallas_call x1, Pallas kernels, pack(): pl.pallas_call(pack_kernel, out_shape=jax.ShapeDtypeStruct((dests, 24, 12...  2.95 us
    pallas_call x1, Pallas kernels, direction_parts(): pl.pallas_call(direction_kernel, out_shape=jax.ShapeDtypeStruct((dests, r...  2.33 us
    pallas_call x1, Pallas kernels, leave(): pl.pallas_call(leave_kernel, out_shape=jax.ShapeDtypeStruct((dests, queri...  2.21 us
    pallas_call x1, Pallas kernels, finish(): pl.pallas_call(finish_kernel, in_specs=[pl.BlockSpec(memory_space=pltpu.S...  1.83 us
  transfers between devices with their start and end apart: 1, of which 0 were waited for; matrix products, arithmetic and copies ran while one was open for 0% of the time, Pallas kernels for 37%

profile of v1, /device:TPU:1, one launch (start us, length us, event | category | flops | bytes accessed | tf_op | source)
XLA Modules:
  0.0 81.4 jit_solution(15759554726786662440)
XLA Ops:
  0.6 1.3 %broadcast_in_dim.2.p_ref = bf16[8,256]{1,0:T(8,128)(2,1)} broadcast(bf16[256]{0:T(256)(128)(2,1)} %param.10), dimensions={1} | broadcast | bytes 4608 | tf_op jit(solution)/shard_map/broadcast_in_dim | solution.py:125
  1.9 2.3 %direction.1 = f32[32,16,128]{2,1,0:T(8,128)} custom-call(bf16[2048,256]{1,0:T(8,128)(2,1)} %w_ref.1, bf16[8,256]{1,0:T(8,128)(2,1)} %broadcast_in_dim.2.p_ref), custom_call_target="tpu_custom_call" | custom-call | flops 1048576 | bytes 1048576 | tf_op jit(solution)/shard_map/direction/pallas_call | solution.py:126
  4.2 9.4 %all-to-all-start = ((f32[32,16,128]{2,1,0:T(8,128)}), f32[32,16,128]{2,1,0:T(8,128)S(1)}, u32[]{:S(2)}, u32[]{:S(2)}) async-start(f32[32,16,128]{2,1,0:T(8,128)} %direction.1), calls=%async_computation | async-start | bytes 524288 | tf_op jit(solution)/shard_map/all_to_all | solution.py:269
  13.6 29.9 %attention.1 = (f32[4,4,512]{2,1,0:T(4,128)}, f32[4,256,512]{2,1,0:T(8,128)}) custom-call(s32[1]{0:T(128)S(6)} %mul.11.base_ref, bf16[64,16,128]{2,1,0:T(8,128)(2,1)} %q_ref.1, bf16[32768,128]{1,0:T(8,128)(2,1)} %bitcast.9, bf16[32768,128]{1,0:T(8,128)(2,1)} %bitcast.10), custom_call_target="tpu_custom_call" | custom-call | flops 17179869184 | bytes 16777216 | tf_op jit(solution)/shard_map/attention/pallas_call | solution.py:83
  43.6 0.0 all-to-all-done.dir_ref
  43.6 0.0 copy-start
  43.6 0.7 copy-done
  44.3 2.9 %pack.1 = f32[32,24,128]{2,1,0:T(8,128)} custom-call(f32[32,16,128]{2,1,0:T(8,128)} %copy-done, f32[4,4,512]{2,1,0:T(4,128)} %get-tuple-element.6.ms_ref, f32[4,256,512]{2,1,0:T(8,128)} %get-tuple-element.7.o_ref), custom_call_target="tpu_custom_call" | custom-call | flops 1048576 | bytes 2097152 | tf_op jit(solution)/shard_map/pack/pallas_call | solution.py:160
  47.2 18.2 %all_to_all.15.got_ref = f32[32,24,128]{2,1,0:T(8,128)} all-to-all(f32[32,24,128]{2,1,0:T(8,128)} %pack.1), channel_id=1, replica_groups=mesh['x'=4,'z'=4,'core'=2,'heads'=4] {'x','z','core'}, dimensions={0} | all-to-all | bytes 786432 | tf_op jit(solution)/shard_map/all_to_all | solution.py:271
  65.4 2.2 %leave.1 = f32[16,16,128]{2,1,0:T(8,128)} custom-call(f32[32,24,128]{2,1,0:T(8,128)} %all_to_all.15.got_ref), custom_call_target="tpu_custom_call" | custom-call | flops 786432 | bytes 393216 | tf_op jit(solution)/shard_map/leave/pallas_call | solution.py:222
  67.6 11.9 %all_to_all.16 = f32[16,16,128]{2,1,0:T(8,128)} all-to-all(f32[16,16,128]{2,1,0:T(8,128)} %leave.1), channel_id=1, replica_groups=mesh['x'=4,'z'=4,'core'=2,'heads'=4] {'x','heads'}, dimensions={0} | all-to-all | bytes 262144 | tf_op jit(solution)/shard_map/all_to_all | solution.py:274
  79.6 1.8 %finish.1 = (f32[4,64]{1,0:T(4,128)}, f32[16,64]{1,0:T(8,128)}) custom-call(s32[1]{0:T(128)} %bitcast.device_ref, f32[4,4,16,128]{3,2,1,0:T(8,128)} %bitcast.7, s32[16,64]{1,0:T(8,128)} %bitcast.8), custom_call_target="tpu_custom_call" | custom-call | tf_op jit(solution)/shard_map/finish/pallas_call | solution.py:251
Async XLA Ops:
  4.2 39.4 %all-to-all-start = ((f32[32,16,128]{2,1,0:T(8,128)}), f32[32,16,128]{2,1,0:T(8,128)S(1)}, u32[]{:S(2)}, u32[]{:S(2)}) async-start(f32[32,16,128]{2,1,0:T(8,128)} %direction.1), calls=%async_computation | async-start | bytes 524288 | tf_op jit(solution)/shard_map/all_to_all | solution.py:269
  43.6 0.7 copy-start

commit v2 on v1

v2 whole, which is shorter than its diff:
```python
import functools

import jax
import jax.numpy as jnp
from jax import lax
from jax.experimental import pallas as pl
from jax.experimental.pallas import tpu as pltpu
from jax.sharding import Mesh, PartitionSpec as P

BLOCK = 4096
KEY_AXES = (4, 4, 2)
NEG = -1e30
SCALE2 = 128 ** -0.5 * 1.4426950408889634
HIGH = lax.Precision.HIGHEST
F32 = jnp.float32


def iota(shape, dim):
    return lax.broadcasted_iota(jnp.int32, shape, dim)


def small(mib):
    return pltpu.CompilerParams(vmem_limit_bytes=mib * 2**20)


def attn_kernel(base_ref, q_hbm, k_hbm, v_hbm, ms_ref, o_ref, q_ref, q_sem, qt, sc, k_ref, v_ref, k_sem, v_sem, *, C, nblk, context, nq):
    total = k_ref.shape[0]
    rows = total // nblk
    R = qt.shape[1]
    hd = k_ref.shape[1]
    per = rows // C
    late = 2 * nq

    def copy(hbm, ref, sem, i):
        at = pl.ds(pl.multiple_of(i * C, C), C)
        return pltpu.make_async_copy(hbm.at[at, :], ref.at[at, :], sem.at[i])

    queries = pltpu.make_async_copy(q_hbm, q_ref, q_sem.at[0])
    queries.start()
    for b in range(nblk):
        for i in range(per):
            copy(k_hbm, k_ref, k_sem, b * per + i).start()
        for i in range(per):
            copy(v_hbm, v_ref, v_sem, b * per + i).start()

    even = (1 - (lax.broadcasted_iota(jnp.int32, (16, hd), 0) & 1)).astype(jnp.bfloat16)
    odd = 1 - even
    lane_even = (1 - (lax.broadcasted_iota(jnp.int32, (16, 128), 1) & 1)).astype(jnp.bfloat16)
    le = jnp.concatenate([lane_even] * (rows // 128), axis=1)[None]

    queries.wait()
    q = q_ref[...].astype(F32)
    g = q.shape[1] // 2
    both = jnp.concatenate([q[:, :g].reshape(R, hd), q[:, g:].reshape(R, hd)], axis=1)
    qt[...] = both.T.astype(jnp.bfloat16)

    def masked(x):
        x3 = x.reshape(x.shape[0] // 16, 16, hd)
        return jnp.concatenate([(x3 * even[None]).reshape(x.shape), (x3 * odd[None]).reshape(x.shape)], axis=1)

    def top_of(s):
        return jnp.max(s.reshape(s.shape[0] // 8, 8, R), axis=0)

    def block(b, carry):
        here = pl.ds(pl.multiple_of(b * rows, rows), rows)
        for c in range(per):
            copy(k_hbm, k_ref, k_sem, b * per + c).wait()
        s = jnp.dot(masked(k_ref[here, :]), qt[...], preferred_element_type=jnp.float32) * SCALE2
        sc[...] = s
        early = top_of(s[:rows - late])

        def seen(_):
            tail = sc[rows - late:, :]
            key = lax.shift_right_logical(iota(tail.shape, 0), 1)
            query = lax.div(iota(tail.shape, 1), jnp.int32(R // nq))
            tail = jnp.where(key <= query, tail, NEG)
            sc[rows - late:, :] = tail
            return top_of(tail)

        last = base_ref[0] + (b + 1) * (rows // 2) == context
        mx = jnp.maximum(early, lax.cond(last, seen, lambda _: top_of(sc[rows - late:, :]), 0))
        mx = jnp.maximum(mx, pltpu.roll(mx, 2, 0))
        mx = jnp.maximum(mx, pltpu.roll(mx, 4, 0))

        for c in range(per):
            copy(v_hbm, v_ref, v_sem, b * per + c).wait()
        p = jnp.exp2(sc[...].reshape(rows // 8, 8, R) - mx[None])
        tot = jnp.sum(p, axis=0)
        pb = p.reshape(rows, R).astype(jnp.bfloat16)
        vt3 = v_ref[here, :].T.reshape(hd // 16, 16, rows)
        vt = jnp.concatenate([(vt3 * le).reshape(hd, rows), (vt3 * (1 - le)).reshape(hd, rows)], axis=0)
        o_ref[b] = jnp.dot(vt, pb, preferred_element_type=jnp.float32)
        tot = tot + pltpu.roll(tot, 2, 0)
        tot = tot + pltpu.roll(tot, 4, 0)
        ms_ref[b, 0:2, :] = mx[0:2]
        ms_ref[b, 2:4, :] = tot[0:2]
        return carry

    lax.fori_loop(0, nblk, block, 0)


def attention(base, queries, keys, values, block, context, C=2048, vl=48):
    nq, hq, hd = queries.shape
    n, kvh, _ = keys.shape
    R = nq * hq // kvh
    nblk = n // block
    rows = kvh * block
    k2 = keys.reshape(n * kvh, hd)
    v2 = values.reshape(n * kvh, hd)
    vmem = pl.BlockSpec(memory_space=pltpu.VMEM)
    hbm = pl.BlockSpec(memory_space=pltpu.HBM)
    return pl.pallas_call(
        functools.partial(attn_kernel, C=C, nblk=nblk, context=context, nq=nq),
        in_specs=[pl.BlockSpec(memory_space=pltpu.SMEM), hbm, hbm, hbm],
        out_specs=[vmem, vmem],
        out_shape=[
            jax.ShapeDtypeStruct((nblk, 4, R), jnp.float32),
            jax.ShapeDtypeStruct((nblk, kvh * hd, R), jnp.float32),
        ],
        scratch_shapes=[
            pltpu.VMEM(queries.shape, jnp.bfloat16),
            pltpu.SemaphoreType.DMA((1,)),
            pltpu.VMEM((kvh * hd, R), jnp.bfloat16),
            pltpu.VMEM((rows, R), jnp.float32),
            pltpu.VMEM((n * kvh, hd), jnp.bfloat16),
            pltpu.VMEM((n * kvh, hd), jnp.bfloat16),
            pltpu.SemaphoreType.DMA((n * kvh // C,)),
            pltpu.SemaphoreType.DMA((n * kvh // C,)),
        ],
        compiler_params=small(vl),
        cost_estimate=pl.CostEstimate(flops=4 * R * n * kvh * hd * 2, bytes_accessed=2 * n * kvh * hd * 2, transcendentals=R * n * kvh),
        name="attention",
    )(base, queries, k2, v2)


def direction_kernel(w_hbm, p_ref, out_ref, w, w_sem):
    copies = []
    step = w.shape[0] // w_sem.shape[0]
    for i in range(w_sem.shape[0]):
        at = pl.ds(i * step, step)
        copies.append(pltpu.make_async_copy(w_hbm.at[at, :], w.at[at, :], w_sem.at[i]))
        copies[-1].start()
    hd = out_ref.shape[2]
    probe = jnp.broadcast_to(p_ref[...].astype(F32).reshape(1, w.shape[1]), (8, w.shape[1])).astype(jnp.bfloat16)
    rows = []
    for i, c in enumerate(copies):
        c.wait()
        part = lax.dot_general(probe, w[i * step:(i + 1) * step, :], (((1,), (1,)), ((), ())), preferred_element_type=F32)
        rows += [part[0:1, h * hd:(h + 1) * hd] for h in range(step // hd)]
    full = jnp.concatenate(rows, axis=0)
    for dest in range(out_ref.shape[0]):
        out_ref[dest] = full


def direction_parts(out_weight, probe, hd, dests):
    rows, cols = out_weight.shape
    vmem = pl.BlockSpec(memory_space=pltpu.VMEM)
    hbm = pl.BlockSpec(memory_space=pltpu.HBM)
    return pl.pallas_call(
        direction_kernel,
        in_specs=[hbm, vmem],
        out_specs=vmem,
        out_shape=jax.ShapeDtypeStruct((dests, rows // hd, hd), F32),
        scratch_shapes=[
            pltpu.VMEM(out_weight.shape, jnp.bfloat16),
            pltpu.SemaphoreType.DMA((4,)),
        ],
        cost_estimate=pl.CostEstimate(flops=2 * rows * cols, bytes_accessed=rows * cols * 2, transcendentals=0),
        compiler_params=small(63),
        name="direction",
    )(out_weight, probe)


def pack_kernel(dir_ref, ms_ref, o_ref, out_ref, x):
    nblk, rows, R = o_ref.shape
    heads, hd = dir_ref.shape[1:]
    group = heads // 2
    direction = jnp.sum(dir_ref[...], axis=0)
    spread = (iota((group, 128), 1) & (group - 1)) == iota((group, 128), 0)
    spread = spread.astype(F32)
    for g in range(2):
        wide = lax.dot_general(direction[g * group:(g + 1) * group], spread, (((0,), (0,)), ((), ())),
                               preferred_element_type=F32, precision=HIGH)
        for b in range(nblk):
            at = g * nblk + b
            x[at:at + 1, :] = ms_ref[b, g:g + 1, :]
            x[8 + at:9 + at, :] = ms_ref[b, 2 + g:3 + g, :]
            for c in range(0, R, 128):
                part = o_ref[b, g * hd:(g + 1) * hd, c:c + 128] * wide
                x[16 + at:17 + at, c:c + 128] = jnp.sum(part, axis=0, keepdims=True)
    total = x[8:16, :]
    level = x[0:8, :] + jnp.log2(total)
    mean = x[16:24, :] / total
    dests = out_ref.shape[0]
    wide = out_ref.shape[2]
    for dest in range(dests):
        c = dest % (R // wide) * wide
        out_ref[dest, 0:8, :] = level[:, c:c + wide]
        out_ref[dest, 8:16, :] = mean[:, c:c + wide]


def pack(gathered, ms, o, shares):
    dests = gathered.shape[0]
    R = ms.shape[2]
    return pl.pallas_call(
        pack_kernel,
        out_shape=jax.ShapeDtypeStruct((dests, 16, R // shares), F32),
        scratch_shapes=[pltpu.VMEM((24, R), F32)],
        cost_estimate=pl.CostEstimate(flops=2 * o.size, bytes_accessed=o.size * 4, transcendentals=0),
        compiler_params=small(8),
        name="pack",
    )(gathered, ms, o)


def turned(x, k):
    row = iota(x.shape, x.ndim - 2) & 3
    return jnp.where(row >= k, pltpu.roll(x, k, x.ndim - 2), pltpu.roll(x, k + 4, x.ndim - 2))


def around(x, op):
    x = op(x, turned(x, 1))
    return op(x, turned(x, 2))


def out_of_sources(x):
    n = x.shape[0]
    before = [jnp.zeros_like(x[0])]
    after = [jnp.zeros_like(x[0])]
    for k in range(n - 1):
        before.append(before[-1] + x[k])
        after.insert(0, after[0] + x[n - 1 - k])
    return jnp.stack([p + q for p, q in zip(before, after)], axis=0)


def leave_kernel(got_ref, out_ref):
    level = got_ref[:, 0:8, :]
    mean = got_ref[:, 8:16, :]
    n, _, lanes = level.shape
    top = around(jnp.max(level, axis=0), jnp.maximum)
    is_top = level == top[None]
    count = around(jnp.sum(is_top.astype(F32), axis=0), jnp.add)
    second = around(jnp.max(jnp.where(is_top, NEG, level), axis=0), jnp.maximum)
    factor = jnp.exp2(level - top[None])
    low = jnp.where(is_top, 0.0, jnp.exp2(jnp.minimum(level - second[None], 0.0)))
    alone = is_top & (count == 1.0)[None]

    def left_out(a, rest):
        inner = turned(a, 1) + turned(a, 2) + turned(a, 3)
        shared = inner + out_of_sources(a + inner)
        rest = around(jnp.sum(rest, axis=0), jnp.add)
        return jnp.where(alone, rest[None], shared)

    ratio = left_out(mean * factor, mean * low) / left_out(factor, low)
    both = ratio + pltpu.roll(ratio, 4, 1)
    pairs = both.reshape(n // 2, 2, 8, lanes)
    dense = jnp.where(iota((n // 2, 8, lanes), 1) < 4, pairs[:, 0], pairs[:, 1]).reshape(n * 4, lanes)
    queries = out_ref.shape[1]
    per = lanes // queries
    pick = lax.div(iota((queries, lanes), 1), jnp.int32(per)) == iota((queries, lanes), 0)
    part = lax.dot_general(pick.astype(F32), dense, (((1,), (1,)), ((), ())), preferred_element_type=F32, precision=HIGH)
    for dest in range(out_ref.shape[0]):
        out_ref[dest] = part


def leave(got, queries, dests):
    return pl.pallas_call(
        leave_kernel,
        out_shape=jax.ShapeDtypeStruct((dests, queries, got.shape[0] * 4), F32),
        cost_estimate=pl.CostEstimate(flops=8 * got.size, bytes_accessed=got.size * 4, transcendentals=got.size),
        compiler_params=small(8),
        name="leave",
    )(got)


def finish_kernel(device_ref, got_ref, knocked_ref, read_ref, pick_ref):
    nx, ny, q, nb = got_ref.shape
    parts = []
    for i in range(nx):
        total = got_ref[i, 0]
        for j in range(1, ny):
            total = total + got_ref[i, j]
        parts.append(total)
    full = jnp.concatenate(parts, axis=0).T
    block = iota(full.shape, 0)
    for k in range(pick_ref.shape[0]):
        here = jnp.where(block == knocked_ref[k:k + 1, :], full, 0.0)
        pick_ref[k:k + 1, :] = jnp.sum(here, axis=0, keepdims=True)
    nblk = read_ref.shape[0]
    for t in range(nblk):
        here = jnp.where(block == device_ref[0] * nblk + t, full, 0.0)
        read_ref[t:t + 1, :] = jnp.sum(here, axis=0, keepdims=True)


def finish(device, got, knocked_t, nblk):
    nx, ny, q, nb = got.shape
    vmem = pl.BlockSpec(memory_space=pltpu.VMEM)
    return pl.pallas_call(
        finish_kernel,
        in_specs=[pl.BlockSpec(memory_space=pltpu.SMEM), vmem, vmem],
        out_specs=[vmem, vmem],
        out_shape=[jax.ShapeDtypeStruct((nblk, nx * q), F32), jax.ShapeDtypeStruct(knocked_t.shape, F32)],
        compiler_params=small(2),
        name="finish",
    )(device, got, knocked_t)


def body(queries, keys, values, out_weight, probe, knocked):
    nq, hq, hd = queries.shape
    nblk = keys.shape[0] // BLOCK
    axes = ("x", "z", "core")
    lanes = lax.axis_size(axes)
    device = lax.axis_index(axes).reshape(1)
    context = keys.shape[0] * lanes
    parts = direction_parts(out_weight, probe, hd, lanes)
    gathered = lax.all_to_all(parts, axes, 0, 0, tiled=True)
    ms, o = attention(device * keys.shape[0], queries, keys, values, BLOCK, context)
    shares, ny = lax.axis_size("core"), lax.axis_size("heads")
    got = lax.all_to_all(pack(gathered, ms, o, shares), axes, 0, 0, tiled=True)
    sent = leave(got, nq // shares, shares * ny)
    back = lax.all_to_all(sent, ("core", "heads"), 0, 0, tiled=True)
    read, picked = finish(device, back.reshape(shares, ny, *back.shape[1:]), knocked.T, nblk)
    return read.T, picked.T


def solution(mesh):
    inner = Mesh(mesh.devices.reshape(*KEY_AXES, mesh.devices.shape[1]), ("x", "z", "core", "heads"))
    keys = ("x", "z", "core")
    in_specs = (
        P(None, "heads", None),
        P(keys, "heads", None),
        P(keys, "heads", None),
        P("heads", keys),
        P(keys),
        P(),
    )
    out_specs = (P(None, keys), P())
    return jax.shard_map(body, mesh=inner, in_specs=in_specs, out_specs=out_specs, check_vma=False)
```

time: 82 us -> 66.4 us (0.81)
  Pallas kernels: 39.2 us -> 26.7 us
  blocking collectives: 30.1 us -> 28.3 us
  local copies, waits for them, and re-layouts: 1.94 us -> 0.95 us
    pallas_call x3, Pallas kernels: 35.2 us -> 24.9 us  [the longest x1 21.3 us: attention(): pl.pallas_call(functools.partial(attn_kernel, C=C, nblk=nblk, context=con...]
    all_to_all x2, blocking collectives: 30.1 us -> 28.3 us  [the longest x1 18.8 us: body(): got = lax.all_to_all(pack(gathered, ms, o, shares), axes, 0, 0, tiled=True)]
    pallas_call x1, Pallas kernels: 2.21 us -> 0.84 us  [leave(): pl.pallas_call(leave_kernel, out_shape=jax.ShapeDtypeStruct((dests, queri...]
    broadcast_in_dim x1 -> x0, local copies, waits for them, and re-layouts: 1.25 us -> none  [direction_parts(): probe8 = jnp.broadcast_to(probe[None], (8, cols))]
    pallas_call x1, Pallas kernels: 1.83 us -> 0.92 us  [finish(): pl.pallas_call(finish_kernel, in_specs=[pl.BlockSpec(memory_space=pltpu.S...]
  transfers between devices with their start and end apart: 1 -> 1, of which waited for: 0 -> 0; matrix products, arithmetic and copies ran while one was open for 0% -> 0% of each run, Pallas kernels for 37% -> 32%
where the time goes in v2:
time: 66.4 us; the launch traced here: 66.1 us
  blocking collectives  28.3 us (43%)
  Pallas kernels  26.7 us (40%)
  starting transfers between devices  9.43 us (14%)
  local copies, waits for them, and re-layouts  0.95 us (1%)
  between operations  0.7 us (1%)
    pallas_call x1, Pallas kernels, attention(): pl.pallas_call(functools.partial(attn_kernel, C=C, nblk=nblk, context=con...  21.3 us
    all_to_all x1, blocking collectives, body(): got = lax.all_to_all(pack(gathered, ms, o, shares), axes, 0, 0, tiled=True)  18.8 us
    all_to_all x1, blocking collectives, body(): back = lax.all_to_all(sent, ('core', 'heads'), 0, 0, tiled=True)  9.57 us
    all_to_all x1, starting transfers between devices, body(): gathered = lax.all_to_all(parts, axes, 0, 0, tiled=True)  9.43 us
    pallas_call x1, Pallas kernels, direction_parts(): pl.pallas_call(direction_kernel, in_specs=[hbm, vmem], out_specs=vmem, ou...  3.08 us
  transfers between devices with their start and end apart: 1, of which 0 were waited for; matrix products, arithmetic and copies ran while one was open for 0% of the time, Pallas kernels for 32%

profile of v2, /device:TPU:1, one launch (start us, length us, event | category | flops | bytes accessed | tf_op | source)
XLA Modules:
  0.0 66.1 jit_solution(4328581306690532119)
XLA Ops:
  0.6 3.1 %direction.1 = f32[32,16,128]{2,1,0:T(8,128)} custom-call(bf16[2048,256]{1,0:T(8,128)(2,1)} %w_hbm.1, bf16[256]{0:T(256)(128)(2,1)} %p_ref.1), custom_call_target="tpu_custom_call" | custom-call | flops 1048576 | bytes 1048576 | tf_op jit(solution)/shard_map/direction/pallas_call | solution.py:159
  3.7 9.4 %all-to-all-start = ((f32[32,16,128]{2,1,0:T(8,128)}), f32[32,16,128]{2,1,0:T(8,128)S(1)}, u32[]{:S(2)}, u32[]{:S(2)}) async-start(f32[32,16,128]{2,1,0:T(8,128)} %direction.1), calls=%async_computation | async-start | bytes 524288 | tf_op jit(solution)/shard_map/all_to_all | solution.py:315
  13.2 0.0 copy-start.1
  13.2 0.9 %copy-done.1 = bf16[64,16,128]{2,1,0:T(8,128)(2,1)S(1)} copy-done((bf16[64,16,128]{2,1,0:T(8,128)(2,1)S(1)}, bf16[64,16,128]{2,1,0:T(8,128)(2,1)}, u32[]{:S(2)}) %copy-start.1) | copy-done | bytes 262168
  14.1 0.0 copy-start
  14.1 21.3 %attention.1 = (f32[4,4,512]{2,1,0:T(4,128)S(1)}, f32[4,256,512]{2,1,0:T(8,128)S(1)}) custom-call(s32[1]{0:T(128)S(6)} %mul.11.base_ref, bf16[64,16,128]{2,1,0:T(8,128)(2,1)S(1)} %copy-done.1, bf16[32768,128]{1,0:T(8,128)(2,1)} %bitcast.9, bf16[32768,128]{1,0:T(8,128)(2,1)} %bitcast.10), custom_call_target="tpu_custom_call" | custom-call | flops 17179869184 | bytes 16777216 | tf_op jit(solution)/shard_map/attention/pallas_call | solution.py:112
  35.5 0.0 all-to-all-done.dir_ref
  35.5 0.5 pack.1
  36.0 18.8 %all_to_all.15.got_ref = f32[32,16,256]{2,1,0:T(8,128)S(1)} all-to-all(f32[32,16,256]{2,1,0:T(8,128)S(1)} %pack.1), channel_id=1, replica_groups=mesh['x'=4,'z'=4,'core'=2,'heads'=4] {'x','z','core'}, dimensions={0} | all-to-all | bytes 1048576 | tf_op jit(solution)/shard_map/all_to_all | solution.py:318
  54.8 0.8 %leave.1 = f32[8,32,128]{2,1,0:T(8,128)S(1)} custom-call(f32[32,16,256]{2,1,0:T(8,128)S(1)} %all_to_all.15.got_ref), custom_call_target="tpu_custom_call" | custom-call | flops 1048576 | bytes 524288 | tf_op jit(solution)/shard_map/leave/pallas_call | solution.py:266
  55.6 9.6 %all_to_all.16 = f32[8,32,128]{2,1,0:T(8,128)S(1)} all-to-all(f32[8,32,128]{2,1,0:T(8,128)S(1)} %leave.1), channel_id=1, replica_groups=mesh['x'=4,'z'=4,'core'=2,'heads'=4] {'core','heads'}, dimensions={0} | all-to-all | bytes 262144 | tf_op jit(solution)/shard_map/all_to_all | solution.py:320
  65.2 0.0 copy-done
  65.2 0.9 %finish.1 = (f32[4,64]{1,0:T(4,128)}, f32[16,64]{1,0:T(8,128)}) custom-call(s32[1]{0:T(128)} %bitcast.device_ref, f32[2,4,32,128]{3,2,1,0:T(8,128)S(1)} %bitcast.7, s32[16,64]{1,0:T(8,128)S(1)} %bitcast.8), custom_call_target="tpu_custom_call" | custom-call | tf_op jit(solution)/shard_map/finish/pallas_call | solution.py:297
Async XLA Ops:
  3.7 31.7 %all-to-all-start = ((f32[32,16,128]{2,1,0:T(8,128)}), f32[32,16,128]{2,1,0:T(8,128)S(1)}, u32[]{:S(2)}, u32[]{:S(2)}) async-start(f32[32,16,128]{2,1,0:T(8,128)} %direction.1), calls=%async_computation | async-start | bytes 524288 | tf_op jit(solution)/shard_map/all_to_all | solution.py:315
  13.2 1.0 %copy-start.1 = (bf16[64,16,128]{2,1,0:T(8,128)(2,1)S(1)}, bf16[64,16,128]{2,1,0:T(8,128)(2,1)}, u32[]{:S(2)}) copy-start(bf16[64,16,128]{2,1,0:T(8,128)(2,1)} %q_hbm.1) | copy-start | bytes 786436
  14.1 51.1 %copy-start = (s32[64,16]{0,1:T(8,128)S(1)}, s32[64,16]{0,1:T(8,128)}, u32[]{:S(2)}) copy-start(s32[64,16]{0,1:T(8,128)} %param.11) | copy-start | bytes 12292

commit v3 on v2

--- a/solution.py
+++ b/solution.py
@@ -20,10 +20,10 @@
 
 
 def small(mib):
-    return pltpu.CompilerParams(vmem_limit_bytes=mib * 2**20)
-
-
-def attn_kernel(base_ref, q_hbm, k_hbm, v_hbm, ms_ref, o_ref, q_ref, q_sem, qt, sc, k_ref, v_ref, k_sem, v_sem, *, C, nblk, context, nq):
+    return pltpu.CompilerParams(vmem_limit_bytes=int(mib * 2**20))
+
+
+def attn_kernel(base_ref, qt, k_hbm, v_hbm, ms_ref, o_ref, sc, k_ref, v_ref, k_sem, v_sem, *, C, nblk, context, nq):
     total = k_ref.shape[0]
     rows = total // nblk
     R = qt.shape[1]
@@ -35,8 +35,6 @@
         at = pl.ds(pl.multiple_of(i * C, C), C)
         return pltpu.make_async_copy(hbm.at[at, :], ref.at[at, :], sem.at[i])
 
-    queries = pltpu.make_async_copy(q_hbm, q_ref, q_sem.at[0])
-    queries.start()
     for b in range(nblk):
         for i in range(per):
             copy(k_hbm, k_ref, k_sem, b * per + i).start()
@@ -47,12 +45,6 @@
     odd = 1 - even
     lane_even = (1 - (lax.broadcasted_iota(jnp.int32, (16, 128), 1) & 1)).astype(jnp.bfloat16)
     le = jnp.concatenate([lane_even] * (rows // 128), axis=1)[None]
-
-    queries.wait()
-    q = q_ref[...].astype(F32)
-    g = q.shape[1] // 2
-    both = jnp.concatenate([q[:, :g].reshape(R, hd), q[:, g:].reshape(R, hd)], axis=1)
-    qt[...] = both.T.astype(jnp.bfloat16)
 
     def masked(x):
         x3 = x.reshape(x.shape[0] // 16, 16, hd)
@@ -99,10 +91,10 @@
     lax.fori_loop(0, nblk, block, 0)
 
 
-def attention(base, queries, keys, values, block, context, C=2048, vl=48):
-    nq, hq, hd = queries.shape
-    n, kvh, _ = keys.shape
-    R = nq * hq // kvh
+def attention(base, qt, keys, values, block, context, nq, vl=48):
+    n, kvh, hd = keys.shape
+    R = qt.shape[1]
+    C = kvh * block
     nblk = n // block
     rows = kvh * block
     k2 = keys.reshape(n * kvh, hd)
@@ -111,16 +103,13 @@
     hbm = pl.BlockSpec(memory_space=pltpu.HBM)
     return pl.pallas_call(
         functools.partial(attn_kernel, C=C, nblk=nblk, context=context, nq=nq),
-        in_specs=[pl.BlockSpec(memory_space=pltpu.SMEM), hbm, hbm, hbm],
+        in_specs=[pl.BlockSpec(memory_space=pltpu.SMEM), vmem, hbm, hbm],
         out_specs=[vmem, vmem],
         out_shape=[
             jax.ShapeDtypeStruct((nblk, 4, R), jnp.float32),
             jax.ShapeDtypeStruct((nblk, kvh * hd, R), jnp.float32),
         ],
         scratch_shapes=[
-            pltpu.VMEM(queries.shape, jnp.bfloat16),
-            pltpu.SemaphoreType.DMA((1,)),
-            pltpu.VMEM((kvh * hd, R), jnp.bfloat16),
             pltpu.VMEM((rows, R), jnp.float32),
             pltpu.VMEM((n * kvh, hd), jnp.bfloat16),
             pltpu.VMEM((n * kvh, hd), jnp.bfloat16),
@@ -130,45 +119,67 @@
         compiler_params=small(vl),
         cost_estimate=pl.CostEstimate(flops=4 * R * n * kvh * hd * 2, bytes_accessed=2 * n * kvh * hd * 2, transcendentals=R * n * kvh),
         name="attention",
-    )(base, queries, k2, v2)
-
-
-def direction_kernel(w_hbm, p_ref, out_ref, w, w_sem):
+    )(base, qt, k2, v2)
+
+
+def direction_kernel(w_hbm, p_hbm, q_hbm, out_hbm, qt_ref, w, p, q, out, sem):
+    count = sem.shape[0] - 3
+    step = w.shape[0] // count
+    first = pltpu.make_async_copy(p_hbm, p, sem.at[count])
+    queries = pltpu.make_async_copy(q_hbm, q, sem.at[count + 1])
+    first.start()
     copies = []
-    step = w.shape[0] // w_sem.shape[0]
-    for i in range(w_sem.shape[0]):
+    for i in range(count):
         at = pl.ds(i * step, step)
-        copies.append(pltpu.make_async_copy(w_hbm.at[at, :], w.at[at, :], w_sem.at[i]))
+        copies.append(pltpu.make_async_copy(w_hbm.at[at, :], w.at[at, :], sem.at[i]))
         copies[-1].start()
-    hd = out_ref.shape[2]
-    probe = jnp.broadcast_to(p_ref[...].astype(F32).reshape(1, w.shape[1]), (8, w.shape[1])).astype(jnp.bfloat16)
+    queries.start()
+    hd = out.shape[2]
+    first.wait()
+    probe = jnp.broadcast_to(p[...].astype(F32).reshape(1, w.shape[1]), (8, w.shape[1])).astype(jnp.bfloat16)
     rows = []
     for i, c in enumerate(copies):
         c.wait()
         part = lax.dot_general(probe, w[i * step:(i + 1) * step, :], (((1,), (1,)), ((), ())), preferred_element_type=F32)
         rows += [part[0:1, h * hd:(h + 1) * hd] for h in range(step // hd)]
     full = jnp.concatenate(rows, axis=0)
-    for dest in range(out_ref.shape[0]):
-        out_ref[dest] = full
-
-
-def direction_parts(out_weight, probe, hd, dests):
+    for dest in range(out.shape[0]):
+        out[dest] = full
+    back = pltpu.make_async_copy(out, out_hbm, sem.at[count + 2])
+    back.start()
+    queries.wait()
+    x = q[...].astype(F32)
+    g = x.shape[1] // 2
+    R = x.shape[0] * g
+    both = jnp.concatenate([x[:, :g].reshape(R, hd), x[:, g:].reshape(R, hd)], axis=1)
+    qt_ref[...] = both.T.astype(jnp.bfloat16)
+    back.wait()
+
+
+def direction_parts(out_weight, probe, queries, dests):
     rows, cols = out_weight.shape
+    nq, hq, hd = queries.shape
     vmem = pl.BlockSpec(memory_space=pltpu.VMEM)
     hbm = pl.BlockSpec(memory_space=pltpu.HBM)
     return pl.pallas_call(
         direction_kernel,
-        in_specs=[hbm, vmem],
-        out_specs=vmem,
-        out_shape=jax.ShapeDtypeStruct((dests, rows // hd, hd), F32),
+        in_specs=[hbm, hbm, hbm],
+        out_specs=[hbm, vmem],
+        out_shape=[
+            jax.ShapeDtypeStruct((dests, rows // hd, hd), F32),
+            jax.ShapeDtypeStruct((2 * hd, nq * hq // 2), jnp.bfloat16),
+        ],
         scratch_shapes=[
             pltpu.VMEM(out_weight.shape, jnp.bfloat16),
-            pltpu.SemaphoreType.DMA((4,)),
+            pltpu.VMEM(probe.shape, jnp.bfloat16),
+            pltpu.VMEM(queries.shape, jnp.bfloat16),
+            pltpu.VMEM((dests, rows // hd, hd), F32),
+            pltpu.SemaphoreType.DMA((7,)),
         ],
         cost_estimate=pl.CostEstimate(flops=2 * rows * cols, bytes_accessed=rows * cols * 2, transcendentals=0),
-        compiler_params=small(63),
+        compiler_params=small(53.25),
         name="direction",
-    )(out_weight, probe)
+    )(out_weight, probe, queries)
 
 
 def pack_kernel(dir_ref, ms_ref, o_ref, out_ref, x):
@@ -311,9 +322,9 @@
     lanes = lax.axis_size(axes)
     device = lax.axis_index(axes).reshape(1)
     context = keys.shape[0] * lanes
-    parts = direction_parts(out_weight, probe, hd, lanes)
+    parts, qt = direction_parts(out_weight, probe, queries, lanes)
     gathered = lax.all_to_all(parts, axes, 0, 0, tiled=True)
-    ms, o = attention(device * keys.shape[0], queries, keys, values, BLOCK, context)
+    ms, o = attention(device * keys.shape[0], qt, keys, values, BLOCK, context, nq)
     shares, ny = lax.axis_size("core"), lax.axis_size("heads")
     got = lax.all_to_all(pack(gathered, ms, o, shares), axes, 0, 0, tiled=True)
     sent = leave(got, nq // shares, shares * ny)

time: 66.4 us -> 64.8 us (0.976)
  Pallas kernels: 26.7 us -> 25.4 us
    pallas_call x1, Pallas kernels: 21.3 us -> 20.6 us  [attention(): pl.pallas_call(functools.partial(attn_kernel, C=C, nblk=nblk, context=con...]
where the time goes in v3:
time: 64.8 us; the launch traced here: 64.5 us
  blocking collectives  28.3 us (44%)
  Pallas kernels  25.4 us (39%)
  starting transfers between devices  9.43 us (15%)
  between operations  0.7 us (1%)
  local copies, waits for them, and re-layouts  0.65 us (1%)
    pallas_call x1, Pallas kernels, attention(): pl.pallas_call(functools.partial(attn_kernel, C=C, nblk=nblk, context=con...  20.6 us
    all_to_all x1, blocking collectives, body(): got = lax.all_to_all(pack(gathered, ms, o, shares), axes, 0, 0, tiled=True)  18.8 us
    all_to_all x1, blocking collectives, body(): back = lax.all_to_all(sent, ('core', 'heads'), 0, 0, tiled=True)  9.57 us
    all_to_all x1, starting transfers between devices, body(): gathered = lax.all_to_all(parts, axes, 0, 0, tiled=True)  9.43 us
    pallas_call x1, Pallas kernels, direction_parts(): pl.pallas_call(direction_kernel, in_specs=[hbm, hbm, hbm], out_specs=[hbm...  2.46 us
  transfers between devices with their start and end apart: 1, of which 0 were waited for; matrix products, arithmetic and copies ran while one was open for 0% of the time, Pallas kernels for 32%

profile of v3, /device:TPU:1, one launch (start us, length us, event | category | flops | bytes accessed | tf_op | source)
XLA Modules:
  0.0 64.5 jit_solution(6865589678858909804)
XLA Ops:
  0.6 0.0 copy-start.1
  0.6 0.6 %copy-done.1 = bf16[256]{0:T(256)(128)(2,1)S(1)} copy-done((bf16[256]{0:T(256)(128)(2,1)S(1)}, bf16[256]{0:T(256)(128)(2,1)}, u32[]{:S(2)}) %copy-start.1) | copy-done | bytes 536
  1.3 2.5 %direction.1 = (f32[32,16,128]{2,1,0:T(8,128)}, bf16[256,512]{1,0:T(8,128)(2,1)S(1)}) custom-call(bf16[2048,256]{1,0:T(8,128)(2,1)} %w_hbm.1, bf16[256]{0:T(256)(128)(2,1)S(1)} %copy-done.1, bf16[64,16,128]{2,1,0:T(8,128)(2,1)} %q_hbm.1), custom_call_target="tpu_custom_call" | custom-call | flops 1048576 | bytes 1048576 | tf_op jit(solution)/shard_map/direction/pallas_call | solution.py:164
  3.8 9.4 %all-to-all-start = ((f32[32,16,128]{2,1,0:T(8,128)}), f32[32,16,128]{2,1,0:T(8,128)S(1)}, u32[]{:S(2)}, u32[]{:S(2)}) async-start(f32[32,16,128]{2,1,0:T(8,128)} %get-tuple-element.8), calls=%async_computation | async-start | bytes 524288 | tf_op jit(solution)/shard_map/all_to_all | solution.py:326
  13.2 0.0 copy-start
  13.2 20.6 %attention.1 = (f32[4,4,512]{2,1,0:T(4,128)S(1)}, f32[4,256,512]{2,1,0:T(8,128)S(1)}) custom-call(s32[1]{0:T(128)S(6)} %mul.11.base_ref, bf16[256,512]{1,0:T(8,128)(2,1)S(1)} %get-tuple-element.9.qt, bf16[32768,128]{1,0:T(8,128)(2,1)} %bitcast.9, bf16[32768,128]{1,0:T(8,128)(2,1)} %bitcast.10), custom_call_target="tpu_custom_call" | custom-call | flops 17179869184 | bytes 16777216 | tf_op jit(solution)/shard_map/attention/pallas_call | solution.py:104
  33.9 0.0 all-to-all-done.dir_ref
  33.9 0.5 pack.1
  34.4 18.8 %all_to_all.15.got_ref = f32[32,16,256]{2,1,0:T(8,128)S(1)} all-to-all(f32[32,16,256]{2,1,0:T(8,128)S(1)} %pack.1), channel_id=1, replica_groups=mesh['x'=4,'z'=4,'core'=2,'heads'=4] {'x','z','core'}, dimensions={0} | all-to-all | bytes 1048576 | tf_op jit(solution)/shard_map/all_to_all | solution.py:329
  53.2 0.8 %leave.1 = f32[8,32,128]{2,1,0:T(8,128)S(1)} custom-call(f32[32,16,256]{2,1,0:T(8,128)S(1)} %all_to_all.15.got_ref), custom_call_target="tpu_custom_call" | custom-call | flops 1048576 | bytes 524288 | tf_op jit(solution)/shard_map/leave/pallas_call | solution.py:277
  54.0 9.6 %all_to_all.16 = f32[8,32,128]{2,1,0:T(8,128)S(1)} all-to-all(f32[8,32,128]{2,1,0:T(8,128)S(1)} %leave.1), channel_id=1, replica_groups=mesh['x'=4,'z'=4,'core'=2,'heads'=4] {'core','heads'}, dimensions={0} | all-to-all | bytes 262144 | tf_op jit(solution)/shard_map/all_to_all | solution.py:331
  63.6 0.0 copy-done
  63.6 0.9 %finish.1 = (f32[4,64]{1,0:T(4,128)}, f32[16,64]{1,0:T(8,128)}) custom-call(s32[1]{0:T(128)} %bitcast.device_ref, f32[2,4,32,128]{3,2,1,0:T(8,128)S(1)} %bitcast.7, s32[16,64]{1,0:T(8,128)S(1)} %bitcast.8), custom_call_target="tpu_custom_call" | custom-call | tf_op jit(solution)/shard_map/finish/pallas_call | solution.py:308
Async XLA Ops:
  0.6 0.7 %copy-start.1 = (bf16[256]{0:T(256)(128)(2,1)S(1)}, bf16[256]{0:T(256)(128)(2,1)}, u32[]{:S(2)}) copy-start(bf16[256]{0:T(256)(128)(2,1)} %p_hbm.1) | copy-start | bytes 1540
  3.8 30.1 %all-to-all-start = ((f32[32,16,128]{2,1,0:T(8,128)}), f32[32,16,128]{2,1,0:T(8,128)S(1)}, u32[]{:S(2)}, u32[]{:S(2)}) async-start(f32[32,16,128]{2,1,0:T(8,128)} %get-tuple-element.8), calls=%async_computation | async-start | bytes 524288 | tf_op jit(solution)/shard_map/all_to_all | solution.py:326
  13.2 50.4 %copy-start = (s32[64,16]{0,1:T(8,128)S(1)}, s32[64,16]{0,1:T(8,128)}, u32[]{:S(2)}) copy-start(s32[64,16]{0,1:T(8,128)} %param.11) | copy-start | bytes 12292

commit v4 on v3

--- a/solution.py
+++ b/solution.py
@@ -174,7 +174,7 @@
             pltpu.VMEM(probe.shape, jnp.bfloat16),
             pltpu.VMEM(queries.shape, jnp.bfloat16),
             pltpu.VMEM((dests, rows // hd, hd), F32),
-            pltpu.SemaphoreType.DMA((7,)),
+            pltpu.SemaphoreType.DMA((5,)),
         ],
         cost_estimate=pl.CostEstimate(flops=2 * rows * cols, bytes_accessed=rows * cols * 2, transcendentals=0),
         compiler_params=small(53.25),

time: 64.8 us -> 64.7 us (level)
  no operation moved by 1% of the time
where the time goes in v4:
time: 64.7 us; the launch traced here: 64.4 us
  blocking collectives  28.3 us (44%)
  Pallas kernels  25.2 us (39%)
  starting transfers between devices  9.43 us (15%)
  between operations  0.7 us (1%)
  local copies, waits for them, and re-layouts  0.65 us (1%)
    pallas_call x1, Pallas kernels, attention(): pl.pallas_call(functools.partial(attn_kernel, C=C, nblk=nblk, context=con...  20.6 us
    all_to_all x1, blocking collectives, body(): got = lax.all_to_all(pack(gathered, ms, o, shares), axes, 0, 0, tiled=True)  18.8 us
    all_to_all x1, blocking collectives, body(): back = lax.all_to_all(sent, ('core', 'heads'), 0, 0, tiled=True)  9.57 us
    all_to_all x1, starting transfers between devices, body(): gathered = lax.all_to_all(parts, axes, 0, 0, tiled=True)  9.43 us
    pallas_call x1, Pallas kernels, direction_parts(): pl.pallas_call(direction_kernel, in_specs=[hbm, hbm, hbm], out_specs=[hbm...  2.3 us
  transfers between devices with their start and end apart: 1, of which 0 were waited for; matrix products, arithmetic and copies ran while one was open for 0% of the time, Pallas kernels for 32%

profile of v4, /device:TPU:1, one launch (start us, length us, event | category | flops | bytes accessed | tf_op | source)
XLA Modules:
  0.0 64.4 jit_solution(8396455646084477398)
XLA Ops:
  0.6 0.0 copy-start.1
  0.6 0.6 %copy-done.1 = bf16[256]{0:T(256)(128)(2,1)S(1)} copy-done((bf16[256]{0:T(256)(128)(2,1)S(1)}, bf16[256]{0:T(256)(128)(2,1)}, u32[]{:S(2)}) %copy-start.1) | copy-done | bytes 536
  1.3 2.3 %direction.1 = (f32[32,16,128]{2,1,0:T(8,128)}, bf16[256,512]{1,0:T(8,128)(2,1)S(1)}) custom-call(bf16[2048,256]{1,0:T(8,128)(2,1)} %w_hbm.1, bf16[256]{0:T(256)(128)(2,1)S(1)} %copy-done.1, bf16[64,16,128]{2,1,0:T(8,128)(2,1)} %q_hbm.1), custom_call_target="tpu_custom_call" | custom-call | flops 1048576 | bytes 1048576 | tf_op jit(solution)/shard_map/direction/pallas_call | solution.py:164
  3.6 9.4 %all-to-all-start = ((f32[32,16,128]{2,1,0:T(8,128)}), f32[32,16,128]{2,1,0:T(8,128)S(1)}, u32[]{:S(2)}, u32[]{:S(2)}) async-start(f32[32,16,128]{2,1,0:T(8,128)} %get-tuple-element.8), calls=%async_computation | async-start | bytes 524288 | tf_op jit(solution)/shard_map/all_to_all | solution.py:326
  13.0 0.0 copy-start
  13.1 20.6 %attention.1 = (f32[4,4,512]{2,1,0:T(4,128)S(1)}, f32[4,256,512]{2,1,0:T(8,128)S(1)}) custom-call(s32[1]{0:T(128)S(6)} %mul.11.base_ref, bf16[256,512]{1,0:T(8,128)(2,1)S(1)} %get-tuple-element.9.qt, bf16[32768,128]{1,0:T(8,128)(2,1)} %bitcast.9, bf16[32768,128]{1,0:T(8,128)(2,1)} %bitcast.10), custom_call_target="tpu_custom_call" | custom-call | flops 17179869184 | bytes 16777216 | tf_op jit(solution)/shard_map/attention/pallas_call | solution.py:104
  33.7 0.0 all-to-all-done.dir_ref
  33.7 0.5 pack.1
  34.2 18.8 %all_to_all.15.got_ref = f32[32,16,256]{2,1,0:T(8,128)S(1)} all-to-all(f32[32,16,256]{2,1,0:T(8,128)S(1)} %pack.1), channel_id=1, replica_groups=mesh['x'=4,'z'=4,'core'=2,'heads'=4] {'x','z','core'}, dimensions={0} | all-to-all | bytes 1048576 | tf_op jit(solution)/shard_map/all_to_all | solution.py:329
  53.0 0.8 %leave.1 = f32[8,32,128]{2,1,0:T(8,128)S(1)} custom-call(f32[32,16,256]{2,1,0:T(8,128)S(1)} %all_to_all.15.got_ref), custom_call_target="tpu_custom_call" | custom-call | flops 1048576 | bytes 524288 | tf_op jit(solution)/shard_map/leave/pallas_call | solution.py:277
  53.9 9.6 %all_to_all.16 = f32[8,32,128]{2,1,0:T(8,128)S(1)} all-to-all(f32[8,32,128]{2,1,0:T(8,128)S(1)} %leave.1), channel_id=1, replica_groups=mesh['x'=4,'z'=4,'core'=2,'heads'=4] {'core','heads'}, dimensions={0} | all-to-all | bytes 262144 | tf_op jit(solution)/shard_map/all_to_all | solution.py:331
  63.4 0.0 copy-done
  63.4 0.9 %finish.1 = (f32[4,64]{1,0:T(4,128)}, f32[16,64]{1,0:T(8,128)}) custom-call(s32[1]{0:T(128)} %bitcast.device_ref, f32[2,4,32,128]{3,2,1,0:T(8,128)S(1)} %bitcast.7, s32[16,64]{1,0:T(8,128)S(1)} %bitcast.8), custom_call_target="tpu_custom_call" | custom-call | tf_op jit(solution)/shard_map/finish/pallas_call | solution.py:308
Async XLA Ops:
  0.6 0.7 %copy-start.1 = (bf16[256]{0:T(256)(128)(2,1)S(1)}, bf16[256]{0:T(256)(128)(2,1)}, u32[]{:S(2)}) copy-start(bf16[256]{0:T(256)(128)(2,1)} %p_hbm.1) | copy-start | bytes 1540
  3.6 30.1 %all-to-all-start = ((f32[32,16,128]{2,1,0:T(8,128)}), f32[32,16,128]{2,1,0:T(8,128)S(1)}, u32[]{:S(2)}, u32[]{:S(2)}) async-start(f32[32,16,128]{2,1,0:T(8,128)} %get-tuple-element.8), calls=%async_computation | async-start | bytes 524288 | tf_op jit(solution)/shard_map/all_to_all | solution.py:326
  13.0 50.4 %copy-start = (s32[64,16]{0,1:T(8,128)S(1)}, s32[64,16]{0,1:T(8,128)}, u32[]{:S(2)}) copy-start(s32[64,16]{0,1:T(8,128)} %param.11) | copy-start | bytes 12292
